TPU v7x, 32 devices: a whole 2x2x4 slice. The times are simulated.
32 devices in a mesh: dp: 4 (over z), row: 2 (over x), col: 4 (over y, core).
Axes of the slice: x: 2, y: 2, z: 4, core: 2. Of those that a mesh axis runs over, the one named last changes fastest.
Arguments:
- grad: bfloat16 [4, 4096, 14336], P('dp', 'row', 'col'), may hold values from -6 to 6
- error: bfloat16 [4, 4096, 14336], P('dp', 'row', 'col'), may hold values from -6 to 6
- q_init: float32 [14336, 128], P('col'), may hold values from -6 to 6
Outputs:
- new_error: bfloat16 [4, 4096, 14336], P('dp', 'row', 'col')
- q_factor: float32 [14336, 128], P('col')
All inputs are finite; a program needn't handle non-finite values.
Results may differ from a plain program's by a relative error of at most 0.001.
Values sent between devices are 32-bit elements; how exact they have to be, the bound alone decides.
A program may use at most 128 MiB of HBM per device.

v0:
```python
import jax
import jax.numpy as jnp
from jax import lax
from jax.sharding import PartitionSpec as P

ITERS = 2


def solve_rows(p_mat, gram):
    lower = jnp.linalg.cholesky(gram)
    return jax.scipy.linalg.solve_triangular(lower, p_mat.T, lower=True).T


def self_gram(p_mat):
    return jnp.dot(
        p_mat.T, p_mat, precision=lax.Precision.HIGHEST, preferred_element_type=jnp.float32
    )


def shards(grad, error, q_init):
    comp = grad[0].astype(jnp.float32) + error[0].astype(jnp.float32)
    scale = 1.0 / lax.axis_size("dp")
    q_mat = q_init
    p_hat = None
    for step in range(ITERS):
        partial_value = jnp.dot(
            comp, q_mat, precision=lax.Precision.HIGHEST, preferred_element_type=jnp.float32
        )
        summed = lax.psum(lax.psum(partial_value, "col"), "dp")
        p_mat = summed * scale
        gram = lax.psum(self_gram(p_mat), "row")
        p_hat = solve_rows(p_mat, gram)
        term = lax.dot_general(
            comp,
            p_hat,
            (((0,), (0,)), ((), ())),
            precision=lax.Precision.HIGHEST,
            preferred_element_type=jnp.float32,
        )
        q_mat = lax.psum(term, ("dp", "row")) * scale
    approx = jnp.dot(
        p_hat, q_mat.T, precision=lax.Precision.HIGHEST, preferred_element_type=jnp.float32
    )
    new_error = (comp - approx).astype(jnp.bfloat16)[None]
    return (new_error, q_mat)


def solution(mesh):
    in_specs = (P("dp", "row", "col"), P("dp", "row", "col"), P("col", None))
    out_specs = (P("dp", "row", "col"), P("col", None))
    return jax.shard_map(shards, mesh=mesh, in_specs=in_specs, out_specs=out_specs, check_vma=False)
```

profile of v0, /device:TPU:0, one launch (start us, length us, event | category | flops | bytes accessed | tf_op | source)
XLA Modules:
  0.0 686.6 jit_solution(13986567056478800305)
XLA Ops:
  7.2 1.4 copy-done
  8.7 28.2 %fusion.6 = f32[2048,128]{1,0:T(8,128)} fusion(f32[3584,128]{1,0:T(8,128)S(1)} %copy-done, bf16[1,2048,3584]{2,1,0:T(8,128)(2,1)} %param.7, bf16[1,2048,3584]{2,1,0:T(8,128)(2,1)} %param.6), kind=kOutput, calls=%fused_computation.7 | convolution fusion | flops 11296309248 | bytes 32243712 | tf_op jit(solution)/shard_map/dot_general | solution.py:26
  37.0 39.1 %all-reduce.9.cloned.1.call-done = f32[2048,128]{1,0:T(8,128)} async-done(((f32[2048,128]{1,0:T(8,128)}), f32[2048,128]{1,0:T(8,128)}) %all-reduce.9.cloned.1.call-update) | async-done | bytes 1048592 | tf_op jit(solution)/shard_map/psum | solution.py:29
  76.2 54.7 %all-reduce.11.cloned.1.call-done = f32[2048,128]{1,0:T(8,128)} async-done(((f32[2048,128]{1,0:T(8,128)}), f32[2048,128]{1,0:T(8,128)}) %all-reduce.11.cloned.1.call-update) | async-done | bytes 1048592 | tf_op jit(solution)/shard_map/psum | solution.py:29
  130.9 4.0 fusion.19
  135.1 20.1 %all-reduce.13.cloned.1.call-done = f32[128,128]{0,1:T(8,128)} async-done(((f32[128,128]{0,1:T(8,128)}), f32[128,128]{0,1:T(8,128)}) %all-reduce.13.cloned.1.call-update) | async-done | bytes 65552 | tf_op jit(solution)/shard_map/psum | solution.py:31
  157.1 11.7 %cholesky.44 = f32[128,128]{1,0:T(8,128)S(1)} custom-call(f32[128,128]{1,0:T(8,128)S(1)} %fusion.31), custom_call_target="Cholesky" | custom-call | tf_op jit(solution)/shard_map/jit(cholesky)/cholesky | solution.py:10
  170.1 9.8 %custom-call.6 = f32[1,128,128]{1,2,0:T(8,128)S(1)} custom-call(f32[1,128,128]{2,1,0:T(8,128)S(1)} %fusion.26), custom_call_target="InvertDiagBlocksLowerTriangular" | custom-call | tf_op jit(solution)/shard_map/jit(_solve_triangular)/triangular_solve | solution.py:11
  179.9 2.3 fusion.13
  182.2 50.6 %fusion.4 = f32[3584,128]{1,0:T(8,128)} fusion(f32[128,2048]{1,0:T(8,128)S(1)} %fusion.13, bf16[1,2048,3584]{2,1,0:T(8,128)(2,1)} %param.7, bf16[1,2048,3584]{2,1,0:T(8,128)(2,1)} %param.6), kind=kOutput, calls=%fused_computation.5 | convolution fusion | flops 11296309248 | bytes 32243712 | tf_op jit(solution)/shard_map/dot_general | solution.py:33
  232.9 95.9 %all-reduce.15.cloned.1.call-done = f32[3584,128]{1,0:T(8,128)} async-done(((f32[3584,128]{1,0:T(8,128)}), f32[3584,128]{1,0:T(8,128)}) %all-reduce.15.cloned.1.call-update) | async-done | bytes 1835024 | tf_op jit(solution)/shard_map/psum | solution.py:40
  328.8 28.4 %fusion.2 = f32[2048,128]{1,0:T(8,128)} fusion(bf16[1,2048,3584]{2,1,0:T(8,128)(2,1)} %param.7, bf16[1,2048,3584]{2,1,0:T(8,128)(2,1)} %param.6, f32[3584,128]{1,0:T(8,128)} %all-reduce.15.cloned.1.call-done), kind=kOutput, calls=%fused_computation.3 | convolution fusion | flops 11296768000 | bytes 32243712 | tf_op jit(solution)/shard_map/dot_general | solution.py:26
  357.3 35.9 %all-reduce.17.cloned.1.call-done = f32[2048,128]{1,0:T(8,128)} async-done(((f32[2048,128]{1,0:T(8,128)}), f32[2048,128]{1,0:T(8,128)}) %all-reduce.17.cloned.1.call-update) | async-done | bytes 1048592 | tf_op jit(solution)/shard_map/psum | solution.py:29
  393.3 54.5 %all-reduce.19.cloned.1.call-done = f32[2048,128]{1,0:T(8,128)} async-done(((f32[2048,128]{1,0:T(8,128)}), f32[2048,128]{1,0:T(8,128)}) %all-reduce.19.cloned.1.call-update) | async-done | bytes 1048592 | tf_op jit(solution)/shard_map/psum | solution.py:29
  447.9 4.0 fusion.16
  452.4 19.9 %all-reduce.21.cloned.1.call-done = f32[128,128]{0,1:T(8,128)} async-done(((f32[128,128]{0,1:T(8,128)}), f32[128,128]{0,1:T(8,128)}) %all-reduce.21.cloned.1.call-update) | async-done | bytes 65552 | tf_op jit(solution)/shard_map/psum | solution.py:31
  472.3 0.9 copy.8
  474.1 11.7 %cholesky.55 = f32[128,128]{1,0:T(8,128)S(1)} custom-call(f32[128,128]{1,0:T(8,128)S(1)} %fusion.29), custom_call_target="Cholesky" | custom-call | tf_op jit(solution)/shard_map/jit(cholesky)/cholesky | solution.py:10
  487.1 9.8 %custom-call.7 = f32[1,128,128]{1,2,0:T(8,128)S(1)} custom-call(f32[1,128,128]{2,1,0:T(8,128)S(1)} %fusion.27), custom_call_target="InvertDiagBlocksLowerTriangular" | custom-call | tf_op jit(solution)/shard_map/jit(_solve_triangular)/triangular_solve | solution.py:11
  496.9 2.3 fusion.11
  499.2 50.5 %fusion = f32[3584,128]{1,0:T(8,128)} fusion(f32[128,2048]{1,0:T(8,128)S(1)} %fusion.11, bf16[1,2048,3584]{2,1,0:T(8,128)(2,1)} %param.7, bf16[1,2048,3584]{2,1,0:T(8,128)(2,1)} %param.6), kind=kOutput, calls=%fused_computation.1 | convolution fusion | flops 11296309248 | bytes 32243712 | tf_op jit(solution)/shard_map/dot_general | solution.py:33
  549.7 96.0 %all-reduce.23.cloned.1.call-done = f32[3584,128]{1,0:T(8,128)} async-done(((f32[3584,128]{1,0:T(8,128)}), f32[3584,128]{1,0:T(8,128)}) %all-reduce.23.cloned.1.call-update) | async-done | bytes 1835024 | tf_op jit(solution)/shard_map/psum | solution.py:40
  645.7 1.6 broadcast_multiply_fusion
  647.3 32.2 %fusion.9 = bf16[1,2048,3584]{2,1,0:T(8,128)(2,1)} fusion(f32[128,2048]{1,0:T(8,128)S(1)} %fusion.11, f32[3584,128]{1,0:T(8,128)S(1)} %broadcast_multiply_fusion, bf16[1,2048,3584]{2,1,0:T(8,128)(2,1)} %param.7, bf16[1,2048,3584]{2,1,0:T(8,128)(2,1)} %param.6), kind=kOutput, calls=%fused_computation.11 | convolution fusion | flops 11310989312 | bytes 46923776 | tf_op jit(solution)/shard_map/dot_general | solution.py:41
  (28 shorter events, 6.4 us)
Async XLA Ops:
  7.2 1.5 copy-start
  7.2 68.9 %all-reduce.9.cloned.1.call-start = ((), (), s32[]{:S(2)}) async-start(), calls=%async_computation | async-start | bytes 2097152 | tf_op jit(solution)/shard_map/psum | solution.py:29
  36.9 93.9 %all-reduce.11.cloned.1.call-start = ((), (), s32[]{:S(2)}) async-start(), calls=%async_computation.1 | async-start | bytes 2097152 | tf_op jit(solution)/shard_map/psum | solution.py:29
  76.1 79.1 %all-reduce.13.cloned.1.call-start = ((), (), s32[]{:S(2)}) async-start(), calls=%async_computation.2 | async-start | bytes 131072 | tf_op jit(solution)/shard_map/psum | solution.py:31
  134.9 193.9 %all-reduce.15.cloned.1.call-start = ((), (), s32[]{:S(2)}) async-start(), calls=%async_computation.3 | async-start | bytes 3670016 | tf_op jit(solution)/shard_map/psum | solution.py:40
  232.9 160.4 %all-reduce.17.cloned.1.call-start = ((), (), s32[]{:S(2)}) async-start(), calls=%async_computation.4 | async-start | bytes 2097152 | tf_op jit(solution)/shard_map/psum | solution.py:29
  357.3 90.6 %all-reduce.19.cloned.1.call-start = ((), (), s32[]{:S(2)}) async-start(), calls=%async_computation.5 | async-start | bytes 2097152 | tf_op jit(solution)/shard_map/psum | solution.py:29
  393.3 79.0 %all-reduce.21.cloned.1.call-start = ((), (), s32[]{:S(2)}) async-start(), calls=%async_computation.6 | async-start | bytes 131072 | tf_op jit(solution)/shard_map/psum | solution.py:31
  451.9 193.8 %all-reduce.23.cloned.1.call-start = ((), (), s32[]{:S(2)}) async-start(), calls=%async_computation.7 | async-start | bytes 3670016 | tf_op jit(solution)/shard_map/psum | solution.py:40
  647.3 32.2 %copy-start.1 = (f32[3584,128]{1,0:T(8,128)}, f32[3584,128]{1,0:T(8,128)S(1)}, u32[]{:S(2)}) copy-start(f32[3584,128]{1,0:T(8,128)S(1)} %broadcast_multiply_fusion) | copy-start | bytes 5505028
Sparse Core Ops, SparseCore 0:
  37.1 39.0 all-reduce.8
  78.5 52.3 all-reduce.10
  135.0 20.1 all-reduce.12
  233.0 95.8 all-reduce.14
  357.4 35.8 all-reduce.16
  395.5 52.3 all-reduce.18
  452.0 20.1 all-reduce.20
  549.8 95.8 all-reduce.22
where the time goes:
time: 693 us; the launch traced here: 687 us
  waiting for transfers between devices  416 us (60%)
  matrix products  203 us (29%)
  other arithmetic  49 us (7%)
  between operations  14.5 us (2%)
    psum x2, waiting for transfers between devices, shards(): q_mat = lax.psum(term, ('dp', 'row')) * scale  192 us
    psum x4, waiting for transfers between devices, shards(): summed = lax.psum(lax.psum(partial_value, 'col'), 'dp')  184 us
    dot_general x2, matrix products, shards(): lax.dot_general(comp, p_hat, (((0,), (0,)), ((), ())), precision=lax.Prec...  101 us
    dot_general x2, matrix products, shards(): jnp.dot(comp, q_mat, precision=lax.Precision.HIGHEST, preferred_element_t...  56.7 us
    psum x2, waiting for transfers between devices, shards(): gram = lax.psum(self_gram(p_mat), 'row')  40 us
    dot_general x1, matrix products, shards(): jnp.dot(p_hat, q_mat.T, precision=lax.Precision.HIGHEST, preferred_elemen...  32.2 us
    another operation x6, other arithmetic, solve_rows(): lower = jnp.linalg.cholesky(gram)  24.8 us
    another operation x4, other arithmetic, solve_rows(): return jax.scipy.linalg.solve_triangular(lower, p_mat.T, lower=True).T  20.9 us
  transfers between devices with their start and end apart: 8, of which 8 were waited for; matrix products, arithmetic and copies ran while one was open for 0% of the time, Pallas kernels for 0%

commit v1 on v0

--- a/solution.py
+++ b/solution.py
@@ -28,7 +28,11 @@
         )
         summed = lax.psum(lax.psum(partial_value, "col"), "dp")
         p_mat = summed * scale
-        gram = lax.psum(self_gram(p_mat), "row")
+
+        def note_the_steps_all(own_rows):
+            return lax.all_gather(own_rows, "row").sum(axis=0)
+
+        gram = note_the_steps_all(self_gram(p_mat))
         p_hat = solve_rows(p_mat, gram)
         term = lax.dot_general(
             comp,

time: 693 us -> 657 us (0.948)
  waiting for transfers between devices: 416 us -> 375 us
  blocking collectives: 0 us -> 10.5 us
    psum x2 -> x0, waiting for transfers between devices: 40 us -> none  [shards(): gram = lax.psum(self_gram(p_mat), 'row')]
    all_gather x0 -> x2, blocking collectives: none -> 10.5 us  [note_the_steps_all(): return lax.all_gather(own_rows, 'row').sum(axis=0)]
  transfers between devices with their start and end apart: 8 -> 6, of which waited for: 8 -> 6; matrix products, arithmetic and copies ran while one was open for 0% -> 0% of each run, Pallas kernels for 0% -> 0%
where the time goes in v1:
time: 657 us; the launch traced here: 651 us
  waiting for transfers between devices  375 us (57%)
  matrix products  202 us (31%)
  other arithmetic  47.4 us (7%)
  between operations  14.4 us (2%)
  blocking collectives  10.5 us (2%)
    psum x2, waiting for transfers between devices, shards(): q_mat = lax.psum(term, ('dp', 'row')) * scale  191 us
    psum x4, waiting for transfers between devices, shards(): summed = lax.psum(lax.psum(partial_value, 'col'), 'dp')  184 us
    dot_general x2, matrix products, shards(): lax.dot_general(comp, p_hat, (((0,), (0,)), ((), ())), precision=lax.Prec...  101 us
    dot_general x2, matrix products, shards(): jnp.dot(comp, q_mat, precision=lax.Precision.HIGHEST, preferred_element_t...  56.7 us
    dot_general x1, matrix products, shards(): jnp.dot(p_hat, q_mat.T, precision=lax.Precision.HIGHEST, preferred_elemen...  32.2 us
    another operation x6, other arithmetic, solve_rows(): lower = jnp.linalg.cholesky(gram)  24.8 us
    another operation x4, other arithmetic, solve_rows(): return jax.scipy.linalg.solve_triangular(lower, p_mat.T, lower=True).T  20.9 us
  transfers between devices with their start and end apart: 6, of which 6 were waited for; matrix products, arithmetic and copies ran while one was open for 0% of the time, Pallas kernels for 0%

profile of v1, /device:TPU:0, one launch (start us, length us, event | category | flops | bytes accessed | tf_op | source)
XLA Modules:
  0.0 650.7 jit_solution(6218776032691773403)
XLA Ops:
  7.2 1.4 copy-done
  8.7 28.2 %fusion.6 = f32[2048,128]{1,0:T(8,128)} fusion(f32[3584,128]{1,0:T(8,128)S(1)} %copy-done, bf16[1,2048,3584]{2,1,0:T(8,128)(2,1)} %param.7, bf16[1,2048,3584]{2,1,0:T(8,128)(2,1)} %param.6), kind=kOutput, calls=%fused_computation.7 | convolution fusion | flops 11296309248 | bytes 32243712 | tf_op jit(solution)/shard_map/dot_general | solution.py:26
  37.0 39.1 %all-reduce.7.cloned.1.call-done = f32[2048,128]{1,0:T(8,128)} async-done(((f32[2048,128]{1,0:T(8,128)}), f32[2048,128]{1,0:T(8,128)}) %all-reduce.7.cloned.1.call-update) | async-done | bytes 1048592 | tf_op jit(solution)/shard_map/psum | solution.py:29
  76.2 54.7 %all-reduce.9.cloned.1.call-done = f32[2048,128]{1,0:T(8,128)} async-done(((f32[2048,128]{1,0:T(8,128)}), f32[2048,128]{1,0:T(8,128)}) %all-reduce.9.cloned.1.call-update) | async-done | bytes 1048592 | tf_op jit(solution)/shard_map/psum | solution.py:29
  130.8 3.5 fusion.19
  134.4 5.1 all-gather
  139.6 11.7 %cholesky.44 = f32[128,128]{1,0:T(8,128)S(1)} custom-call(f32[128,128]{1,0:T(8,128)S(1)} %fusion.31), custom_call_target="Cholesky" | custom-call | tf_op jit(solution)/shard_map/jit(cholesky)/cholesky | solution.py:10
  152.0 0.7 fusion.26
  152.6 9.8 %custom-call.6 = f32[1,128,128]{1,2,0:T(8,128)S(1)} custom-call(f32[1,128,128]{2,1,0:T(8,128)S(1)} %fusion.26), custom_call_target="InvertDiagBlocksLowerTriangular" | custom-call | tf_op jit(solution)/shard_map/jit(_solve_triangular)/triangular_solve | solution.py:11
  162.5 2.3 fusion.13
  164.8 50.6 %fusion.4 = f32[3584,128]{1,0:T(8,128)} fusion(f32[128,2048]{1,0:T(8,128)S(1)} %fusion.13, bf16[1,2048,3584]{2,1,0:T(8,128)(2,1)} %param.7, bf16[1,2048,3584]{2,1,0:T(8,128)(2,1)} %param.6), kind=kOutput, calls=%fused_computation.5 | convolution fusion | flops 11296309248 | bytes 32243712 | tf_op jit(solution)/shard_map/dot_general | solution.py:37
  215.5 95.3 %all-reduce.11.cloned.1.call-done = f32[3584,128]{1,0:T(8,128)} async-done(((f32[3584,128]{1,0:T(8,128)}), f32[3584,128]{1,0:T(8,128)}) %all-reduce.11.cloned.1.call-update) | async-done | bytes 1835024 | tf_op jit(solution)/shard_map/psum | solution.py:44
  310.7 28.4 %fusion.2 = f32[2048,128]{1,0:T(8,128)} fusion(bf16[1,2048,3584]{2,1,0:T(8,128)(2,1)} %param.7, bf16[1,2048,3584]{2,1,0:T(8,128)(2,1)} %param.6, f32[3584,128]{1,0:T(8,128)} %all-reduce.11.cloned.1.call-done), kind=kOutput, calls=%fused_computation.3 | convolution fusion | flops 11296768000 | bytes 32243712 | tf_op jit(solution)/shard_map/dot_general | solution.py:26
  339.2 35.9 %all-reduce.13.cloned.1.call-done = f32[2048,128]{1,0:T(8,128)} async-done(((f32[2048,128]{1,0:T(8,128)}), f32[2048,128]{1,0:T(8,128)}) %all-reduce.13.cloned.1.call-update) | async-done | bytes 1048592 | tf_op jit(solution)/shard_map/psum | solution.py:29
  375.2 54.5 %all-reduce.15.cloned.1.call-done = f32[2048,128]{1,0:T(8,128)} async-done(((f32[2048,128]{1,0:T(8,128)}), f32[2048,128]{1,0:T(8,128)}) %all-reduce.15.cloned.1.call-update) | async-done | bytes 1048592 | tf_op jit(solution)/shard_map/psum | solution.py:29
  429.7 3.5 fusion.16
  433.3 5.4 all-gather.1
  438.8 11.7 %cholesky.55 = f32[128,128]{1,0:T(8,128)S(1)} custom-call(f32[128,128]{1,0:T(8,128)S(1)} %fusion.29), custom_call_target="Cholesky" | custom-call | tf_op jit(solution)/shard_map/jit(cholesky)/cholesky | solution.py:10
  451.8 9.8 %custom-call.7 = f32[1,128,128]{1,2,0:T(8,128)S(1)} custom-call(f32[1,128,128]{2,1,0:T(8,128)S(1)} %fusion.27), custom_call_target="InvertDiagBlocksLowerTriangular" | custom-call | tf_op jit(solution)/shard_map/jit(_solve_triangular)/triangular_solve | solution.py:11
  461.7 2.3 fusion.11
  464.0 50.5 %fusion = f32[3584,128]{1,0:T(8,128)} fusion(f32[128,2048]{1,0:T(8,128)S(1)} %fusion.11, bf16[1,2048,3584]{2,1,0:T(8,128)(2,1)} %param.7, bf16[1,2048,3584]{2,1,0:T(8,128)(2,1)} %param.6), kind=kOutput, calls=%fused_computation.1 | convolution fusion | flops 11296309248 | bytes 32243712 | tf_op jit(solution)/shard_map/dot_general | solution.py:37
  514.4 95.3 %all-reduce.17.cloned.1.call-done = f32[3584,128]{1,0:T(8,128)} async-done(((f32[3584,128]{1,0:T(8,128)}), f32[3584,128]{1,0:T(8,128)}) %all-reduce.17.cloned.1.call-update) | async-done | bytes 1835024 | tf_op jit(solution)/shard_map/psum | solution.py:44
  609.7 1.6 broadcast_multiply_fusion
  611.4 32.2 %fusion.9 = bf16[1,2048,3584]{2,1,0:T(8,128)(2,1)} fusion(f32[128,2048]{1,0:T(8,128)S(1)} %fusion.11, f32[3584,128]{1,0:T(8,128)S(1)} %broadcast_multiply_fusion, bf16[1,2048,3584]{2,1,0:T(8,128)(2,1)} %param.7, bf16[1,2048,3584]{2,1,0:T(8,128)(2,1)} %param.6), kind=kOutput, calls=%fused_computation.11 | convolution fusion | flops 11310989312 | bytes 46923776 | tf_op jit(solution)/shard_map/dot_general | solution.py:45
  (26 shorter events, 2.6 us)
Async XLA Ops:
  7.2 1.5 copy-start
  7.2 68.9 %all-reduce.7.cloned.1.call-start = ((), (), s32[]{:S(2)}) async-start(), calls=%async_computation | async-start | bytes 2097152 | tf_op jit(solution)/shard_map/psum | solution.py:29
  36.9 93.9 %all-reduce.9.cloned.1.call-start = ((), (), s32[]{:S(2)}) async-start(), calls=%async_computation.1 | async-start | bytes 2097152 | tf_op jit(solution)/shard_map/psum | solution.py:29
  76.1 234.6 %all-reduce.11.cloned.1.call-start = ((), (), s32[]{:S(2)}) async-start(), calls=%async_computation.2 | async-start | bytes 3670016 | tf_op jit(solution)/shard_map/psum | solution.py:44
  215.4 159.7 %all-reduce.13.cloned.1.call-start = ((), (), s32[]{:S(2)}) async-start(), calls=%async_computation.3 | async-start | bytes 2097152 | tf_op jit(solution)/shard_map/psum | solution.py:29
  339.2 90.6 %all-reduce.15.cloned.1.call-start = ((), (), s32[]{:S(2)}) async-start(), calls=%async_computation.4 | async-start | bytes 2097152 | tf_op jit(solution)/shard_map/psum | solution.py:29
  375.2 234.6 %all-reduce.17.cloned.1.call-start = ((), (), s32[]{:S(2)}) async-start(), calls=%async_computation.5 | async-start | bytes 3670016 | tf_op jit(solution)/shard_map/psum | solution.py:44
  611.4 32.2 %copy-start.1 = (f32[3584,128]{1,0:T(8,128)}, f32[3584,128]{1,0:T(8,128)S(1)}, u32[]{:S(2)}) copy-start(f32[3584,128]{1,0:T(8,128)S(1)} %broadcast_multiply_fusion) | copy-start | bytes 5505028
Sparse Core Ops, SparseCore 0:
  37.1 38.9 all-reduce.6
  78.4 52.3 all-reduce.8
  215.5 95.1 all-reduce.10
  339.3 35.8 all-reduce.12
  377.4 52.3 all-reduce.14
  514.6 95.1 all-reduce.16
